TPU v7x, 32 devices: a whole 2x2x4 slice. The times are simulated.
32 devices in a mesh: grp: 2 (over core), tp: 4 (over y, x), src: 4 (over z).
Axes of the slice: x: 2, y: 2, z: 4, core: 2. Of those that a mesh axis runs over, the one named last changes fastest.
Arguments:
- hidden_in: bfloat16 [512, 5120], P(('grp', 'src')), may hold values from -6 to 6
- attn_gain: float32 [5120], replicated, may hold values from 0.5 to 1.5
- w_qkv: int32 [1280, 5120], P(None, 'tp'), may hold values from -2147483648 to 2147483646
- qkv_scale: float32 [5120], P('tp'), may hold values from 0.0001118034 to 0.00041926274
- q_gain: float32 [128], replicated, may hold values from 0.25 to 1.75
- k_gain: float32 [128], replicated, may hold values from 0.1 to 1.9
- key_cache: bfloat16 [8, 64, 128, 512], P(('grp', 'src'), 'tp'), may hold values from -400 to 400
- value_cache: bfloat16 [8, 64, 128, 512], P(('grp', 'src'), 'tp'), may hold values from -9 to 9
- lengths: int32 [8, 64], P(('grp', 'src'), 'tp'), may hold values from 1 to 128, as said below
- w_out: int32 [1024, 5120], P('tp'), may hold values from -2147483648 to 2147483646
- out_scale: float32 [5120], replicated, may hold values from 0.0003125 to 0.00125
- mlp_gain: float32 [5120], replicated, may hold values from 0.5 to 1.5
- w_gate: int32 [1280, 12800], P(('grp', 'src'), 'tp'), may hold values from -2147483648 to 2147483646
- w_up: int32 [1280, 12800], P(('grp', 'src'), 'tp'), may hold values from -2147483648 to 2147483646
- gate_scale: float32 [12800], P('tp'), may hold values from 0.0001118034 to 0.00041926274
- up_scale: float32 [12800], P('tp'), may hold values from 0.0001118034 to 0.00041926274
- w_down: int32 [3200, 5120], P('tp', ('grp', 'src')), may hold values from -2147483648 to 2147483646
- down_scale: float32 [5120], replicated, may hold values from 0.00013258251 to 0.00053033006
Outputs:
- layer_out: bfloat16 [512, 5120], P(('grp', 'src'), 'tp')
Inputs may be any that keep to these rules, and one draw needn't show every extreme that they name: `lengths`: some sequence has exactly 128 cached positions.
All inputs are finite; a program needn't handle non-finite values.
Results may differ from a plain program's by a relative error of at most 0.028.
Values may be sent and summed in bfloat16 or wider, within the bound.
A program may use at most 128 MiB of HBM per device.

v0:
```python
import math
import jax
import jax.numpy as jnp
from jax import lax
from jax.sharding import PartitionSpec as P

D = 5120
QUERY_HEADS = 32
KEY_VALUE_HEADS = 4
HEAD_SIZE = 128
QUERY_COLUMNS = 4096
KEY_COLUMNS = 512
norm_epsilon = 1e-06
rope_base = 1000000.0


def unpack_bytes(packed, byte_index):
    return jnp.right_shift(jnp.left_shift(packed, 24 - 8 * byte_index), 24)


def byte_product(activations, packed):
    products = [
        jnp.dot(
            activations[:, byte_index::4],
            unpack_bytes(packed, byte_index).astype(jnp.bfloat16),
            preferred_element_type=jnp.float32,
        )
        for byte_index in range(4)
    ]
    return products[0] + products[1] + products[2] + products[3]


def normalize_rows(values, gain_row):
    return (
        values
        * lax.rsqrt(jnp.mean(values * values, axis=-1, keepdims=True) + norm_epsilon)
        * gain_row
    )


def rotary_embed(values, positions):
    half_dim = values.shape[-1] // 2
    freq_index = jnp.arange(half_dim, dtype=jnp.float32)
    inverse = jnp.exp(freq_index * (-math.log(rope_base) / half_dim))
    angles = positions.astype(jnp.float32)[:, None] * inverse[None, :]
    cosine = jnp.cos(angles)[:, None, :]
    sine_part = jnp.sin(angles)[:, None, :]
    lower_half = values[..., :half_dim]
    upper_half = values[..., half_dim:]
    return jnp.concatenate(
        [
            lower_half * cosine - upper_half * sine_part,
            upper_half * cosine + lower_half * sine_part,
        ],
        axis=-1,
    )


def local_attention(query_key_value_rows, q_gain, k_gain, stored_keys, stored_values, seq_lengths):
    count_of_rows = query_key_value_rows.shape[0]
    cache_length = stored_keys.shape[1]
    query_matrix = (
        query_key_value_rows[:, :QUERY_COLUMNS]
        .astype(jnp.float32)
        .reshape(count_of_rows, QUERY_HEADS, HEAD_SIZE)
    )
    incoming_keys = (
        query_key_value_rows[:, QUERY_COLUMNS : QUERY_COLUMNS + KEY_COLUMNS]
        .astype(jnp.float32)
        .reshape(count_of_rows, KEY_VALUE_HEADS, HEAD_SIZE)
    )
    incoming_values = query_key_value_rows[:, QUERY_COLUMNS + KEY_COLUMNS :].reshape(
        count_of_rows, KEY_VALUE_HEADS, HEAD_SIZE
    )
    query_matrix = rotary_embed(normalize_rows(query_matrix, q_gain), seq_lengths).astype(
        jnp.bfloat16
    )
    incoming_keys = rotary_embed(normalize_rows(incoming_keys, k_gain), seq_lengths).astype(
        jnp.bfloat16
    )
    query_groups = query_matrix.reshape(
        count_of_rows, KEY_VALUE_HEADS, QUERY_HEADS // KEY_VALUE_HEADS, HEAD_SIZE
    )
    key_slices = stored_keys.reshape(count_of_rows, cache_length, KEY_VALUE_HEADS, HEAD_SIZE)
    value_slices = stored_values.reshape(count_of_rows, cache_length, KEY_VALUE_HEADS, HEAD_SIZE)
    logit_scale = 1.0 / math.sqrt(HEAD_SIZE)
    scores = (
        jnp.einsum("bkgd,bpkd->bkgp", query_groups, key_slices, preferred_element_type=jnp.float32)
        * logit_scale
    )
    live_mask = jnp.arange(cache_length, dtype=jnp.int32)[None, :] < seq_lengths[:, None]
    scores = jnp.where(live_mask[:, None, None, :], scores, -jnp.inf)
    self_score = (
        jnp.einsum("nufi,nui->nuf", query_groups, incoming_keys, preferred_element_type=jnp.float32)
        * logit_scale
    )
    row_max = jnp.maximum(jnp.max(scores, axis=-1), self_score)
    soft_weights = jnp.exp(scores - row_max[..., None])
    own_weight = jnp.exp(self_score - row_max)
    denominator = jnp.sum(soft_weights, axis=-1) + own_weight
    own_low = lax.optimization_barrier(own_weight.astype(jnp.bfloat16)).astype(jnp.float32)
    numerator = jnp.einsum(
        "bkgp,bpkd->bkgd",
        soft_weights.astype(jnp.bfloat16),
        value_slices,
        preferred_element_type=jnp.float32,
    )
    numerator = numerator + own_low[..., None] * incoming_values.astype(jnp.float32)[:, :, None, :]
    return (
        (numerator / denominator[..., None])
        .reshape(count_of_rows, QUERY_COLUMNS)
        .astype(jnp.bfloat16)
    )


def local(
    hidden_in,
    attn_gain,
    w_qkv,
    qkv_scale,
    q_gain,
    k_gain,
    key_cache,
    value_cache,
    lengths,
    w_out,
    out_scale,
    mlp_gain,
    w_gate,
    w_up,
    gate_scale,
    up_scale,
    w_down,
    down_scale,
):
    tp_count = lax.axis_size("tp")
    tp_index = lax.axis_index("tp")
    share_cols = D // tp_count
    residual = hidden_in.astype(jnp.float32)
    normed = normalize_rows(residual, attn_gain).astype(jnp.bfloat16)
    qkv_part = (byte_product(normed, w_qkv) * qkv_scale).astype(jnp.bfloat16)
    query_key_value_rows = lax.all_to_all(qkv_part, "tp", split_axis=0, concat_axis=1, tiled=True)
    heads_out = local_attention(
        query_key_value_rows, q_gain, k_gain, key_cache[0], value_cache[0], lengths[0]
    )
    head_rows = lax.all_to_all(heads_out, "tp", split_axis=1, concat_axis=0, tiled=True)
    partial_value = byte_product(head_rows, w_out) * out_scale
    attn_full = lax.psum(partial_value.astype(jnp.bfloat16), "tp").astype(jnp.float32)
    mid_full = (residual + attn_full).astype(jnp.bfloat16)
    normed_mlp = normalize_rows(mid_full.astype(jnp.float32), mlp_gain).astype(jnp.bfloat16)
    mid_share = lax.dynamic_slice_in_dim(mid_full, tp_index * share_cols, share_cols, 1)
    gate_total = byte_product(
        normed_mlp, lax.all_gather(w_gate, ("grp", "src"), axis=0, tiled=True)
    )
    up_total = byte_product(normed_mlp, lax.all_gather(w_up, ("grp", "src"), axis=0, tiled=True))
    activated = (jax.nn.silu(gate_total * gate_scale) * (up_total * up_scale)).astype(jnp.bfloat16)
    down_terms = (
        byte_product(activated, lax.all_gather(w_down, ("grp", "src"), axis=1, tiled=True))
        * down_scale
    )
    mlp_share = lax.psum_scatter(
        down_terms.astype(jnp.bfloat16), "tp", scatter_dimension=1, tiled=True
    ).astype(jnp.float32)
    return (mid_share.astype(jnp.float32) + mlp_share).astype(jnp.bfloat16)


def solution(mesh):
    return jax.shard_map(
        local,
        mesh=mesh,
        in_specs=(
            P(("grp", "src"), None),
            P(),
            P(None, "tp"),
            P("tp"),
            P(),
            P(),
            P(("grp", "src"), "tp", None, None),
            P(("grp", "src"), "tp", None, None),
            P(("grp", "src"), "tp"),
            P("tp", None),
            P(),
            P(),
            P(("grp", "src"), "tp"),
            P(("grp", "src"), "tp"),
            P("tp"),
            P("tp"),
            P("tp", ("grp", "src")),
            P(),
        ),
        out_specs=P(("grp", "src"), "tp"),
        check_vma=False,
    )
```

profile of v0, /device:TPU:0, one launch (start us, length us, event | category | flops | bytes accessed | tf_op | source)
XLA Modules:
  0.0 582.0 jit_solution(6829318386932394782)
XLA Ops:
  10.0 6.5 %slice.73 = bf16[64,1280]{1,0:T(8,128)(2,1)S(1)} slice(bf16[64,5120]{1,0:T(8,128)(2,1)S(1)} %fusion.83), slice={[0:64:1], [0:5120:4]} | slice | bytes 327680 | tf_op jit(solution)/shard_map/slice | solution.py:24
  16.6 6.6 %slice.74 = bf16[64,1280]{1,0:T(8,128)(2,1)S(1)} slice(bf16[64,5120]{1,0:T(8,128)(2,1)S(1)} %fusion.83), slice={[0:64:1], [1:5120:4]} | slice | bytes 327680 | tf_op jit(solution)/shard_map/slice | solution.py:24
  23.1 6.5 %slice.75 = bf16[64,1280]{1,0:T(8,128)(2,1)S(1)} slice(bf16[64,5120]{1,0:T(8,128)(2,1)S(1)} %fusion.83), slice={[0:64:1], [2:5120:4]} | slice | bytes 327680 | tf_op jit(solution)/shard_map/slice | solution.py:24
  29.6 6.7 %slice.76 = bf16[64,1280]{1,0:T(8,128)(2,1)S(1)} slice(bf16[64,5120]{1,0:T(8,128)(2,1)S(1)} %fusion.83), slice={[0:64:1], [3:5120:4]} | slice | bytes 327680 | tf_op jit(solution)/shard_map/slice | solution.py:24
  36.4 4.0 fusion.50
  44.8 5.3 all-to-all-start
  52.7 4.0 reshape_squeeze.7
  62.3 9.2 %all_to_all.35 = bf16[16,4,1024]{2,0,1:T(8,128)(2,1)S(1)} all-to-all(bf16[16,4,1024]{2,0,1:T(8,128)(2,1)S(1)} %copy.28), channel_id=1, replica_groups=mesh['grp'=2,'tp'=4,'src'=4] {'tp'}, dimensions={1} | all-to-all | bytes 262144 | tf_op jit(solution)/shard_map/all_to_all | solution.py:146
  87.5 44.9 %all-reduce.2.cloned.1.call-done = bf16[64,5120]{1,0:T(8,128)(2,1)} async-done(((bf16[64,5120]{1,0:T(8,128)(2,1)}), bf16[64,5120]{1,0:T(8,128)(2,1)}) %all-reduce.2.cloned.1.call-update) | async-done | bytes 655376 | tf_op jit(solution)/shard_map/psum | solution.py:148
  134.0 7.0 %slice.88 = bf16[64,1280]{1,0:T(8,128)(2,1)S(1)} slice(bf16[64,5120]{1,0:T(8,128)(2,1)S(1)} %fusion.80), slice={[0:64:1], [0:5120:4]} | slice | bytes 327680 | tf_op jit(solution)/shard_map/slice | solution.py:24
  141.0 6.6 %slice.89 = bf16[64,1280]{1,0:T(8,128)(2,1)S(1)} slice(bf16[64,5120]{1,0:T(8,128)(2,1)S(1)} %fusion.80), slice={[0:64:1], [1:5120:4]} | slice | bytes 327680 | tf_op jit(solution)/shard_map/slice | solution.py:24
  147.6 6.5 %slice.90 = bf16[64,1280]{1,0:T(8,128)(2,1)S(1)} slice(bf16[64,5120]{1,0:T(8,128)(2,1)S(1)} %fusion.80), slice={[0:64:1], [2:5120:4]} | slice | bytes 327680 | tf_op jit(solution)/shard_map/slice | solution.py:24
  154.1 6.7 %slice.91 = bf16[64,1280]{1,0:T(8,128)(2,1)S(1)} slice(bf16[64,5120]{1,0:T(8,128)(2,1)S(1)} %fusion.80), slice={[0:64:1], [3:5120:4]} | slice | bytes 327680 | tf_op jit(solution)/shard_map/slice | solution.py:24
  160.8 74.5 %all-gather.4.cloned.1.call-done = s32[1280,3200]{1,0:T(8,128)} async-done(((s32[160,3200]{1,0:T(8,128)}), s32[1280,3200]{1,0:T(8,128)}) %all-gather.4.cloned.1.call-update) | async-done | bytes 16384016 | tf_op jit(solution)/shard_map/all_gather | solution.py:153
  235.3 8.0 %fusion = f32[64,3200]{1,0:T(8,128)S(1)} fusion(bf16[64,1280]{1,0:T(8,128)(2,1)S(1)} %slice.88, s32[1280,3200]{1,0:T(8,128)} %all-gather.4.cloned.1.call-done), kind=kOutput, calls=%fused_computation.12 | convolution fusion | flops 536576000 | bytes 17367040 | tf_op jit(solution)/shard_map/dot_general | solution.py:23
  243.3 139.4 %all-gather.6.cloned.1.call-done = s32[1280,3200]{1,0:T(8,128)} async-done(((s32[160,3200]{1,0:T(8,128)}), s32[1280,3200]{1,0:T(8,128)}) %all-gather.6.cloned.1.call-update) | async-done | bytes 16384016 | tf_op jit(solution)/shard_map/all_gather | solution.py:155
  382.7 8.1 %fusion.4 = f32[64,3200]{1,0:T(8,128)S(1)} fusion(bf16[64,1280]{1,0:T(8,128)(2,1)S(1)} %slice.88, s32[1280,3200]{1,0:T(8,128)} %all-gather.6.cloned.1.call-done), kind=kOutput, calls=%fused_computation.16 | convolution fusion | flops 536576000 | bytes 17367040 | tf_op jit(solution)/shard_map/dot_general | solution.py:23
  390.8 9.9 %fusion.45 = f32[64,3200]{1,0:T(8,128)S(1)} fusion(f32[64,3200]{1,0:T(8,128)S(1)} %fusion, bf16[64,1280]{1,0:T(8,128)(2,1)S(1)} %slice.89, s32[1280,3200]{1,0:T(8,128)} %all-gather.4.cloned.1.call-done), kind=kOutput, calls=%fused_computation.68 | convolution fusion | flops 536780800 | bytes 18186240 | tf_op jit(solution)/shard_map/dot_general | solution.py:23
  403.2 8.0 %fusion.44 = f32[64,3200]{1,0:T(8,128)S(1)} fusion(f32[64,3200]{1,0:T(8,128)S(1)} %fusion.45, bf16[64,1280]{1,0:T(8,128)(2,1)S(1)} %slice.90, s32[1280,3200]{1,0:T(8,128)} %all-gather.4.cloned.1.call-done), kind=kOutput, calls=%fused_computation.67 | convolution fusion | flops 536780800 | bytes 18186240 | tf_op jit(solution)/shard_map/dot_general | solution.py:23
  413.9 7.6 %fusion.46 = f32[64,3200]{1,0:T(8,128)S(1)} fusion(f32[64,3200]{1,0:T(8,128)S(1)} %fusion.44, bf16[64,1280]{1,0:T(8,128)(2,1)S(1)} %slice.91, s32[1280,3200]{1,0:T(8,128)} %all-gather.4.cloned.1.call-done, f32[3200]{0:T(1024)S(1)} %copy-done.7), kind=kOutput, calls=%fused_computation.69 | convolution fusion | flops 536985600 | bytes 18199040 | tf_op jit(solution)/shard_map/dot_general | solution.py:23
  434.6 4.0 slice.95
  438.6 91.5 %all-gather.8.cloned.1.call-done = s32[800,5120]{1,0:T(8,128)} async-done(((s32[800,640]{1,0:T(8,128)}), s32[800,5120]{1,0:T(8,128)}) %all-gather.8.cloned.1.call-update) | async-done | bytes 16384016 | tf_op jit(solution)/shard_map/all_gather | solution.py:158
  530.1 8.2 %fusion.8 = f32[64,5120]{1,0:T(8,128)S(1)} fusion(bf16[64,800]{1,0:T(8,128)(2,1)S(1)} %slice.92, s32[800,5120]{1,0:T(8,128)} %all-gather.8.cloned.1.call-done), kind=kOutput, calls=%fused_computation.20 | convolution fusion | flops 536576000 | bytes 17797120 | tf_op jit(solution)/shard_map/dot_general | solution.py:23
  548.3 24.0 %reduce-scatter.2.cloned.1.call-done = bf16[64,1280]{1,0:T(8,128)(2,1)} async-done(((bf16[64,5120]{1,0:T(8,128)(2,1)}), bf16[64,1280]{1,0:T(8,128)(2,1)}) %reduce-scatter.2.cloned.1.call-update) | async-done | bytes 163856 | tf_op jit(solution)/shard_map/reduce_scatter | solution.py:161
  (105 shorter events, 62.2 us)
Async XLA Ops:
  36.4 4.7 copy-start.1
  41.1 2.1 copy-start.8
  42.2 8.0 %copy-start.11 = (s32[1,16]{1,0:T(1,128)S(1)}, s32[1,16]{1,0:T(1,128)}, u32[]{:S(2)}) copy-start(s32[1,16]{1,0:T(1,128)} %param.26) | copy-start | bytes 196
  44.8 12.5 %copy-start.9 = (f32[128]{0:T(128)S(1)}, f32[128]{0:T(128)}, u32[]{:S(2)}) copy-start(f32[128]{0:T(128)} %param.23) | copy-start | bytes 1540
  44.8 12.6 %copy-start.10 = (f32[128]{0:T(128)S(1)}, f32[128]{0:T(128)}, u32[]{:S(2)}) copy-start(f32[128]{0:T(128)} %param.22) | copy-start | bytes 1540
  44.8 12.1 %all-to-all-start = ((bf16[4,16,1280]{2,1,0:T(8,128)(2,1)}), bf16[4,16,1280]{2,1,0:T(8,128)(2,1)S(1)}, u32[]{:S(2)}, u32[]{:S(2)}) async-start(bf16[4,16,1280]{2,1,0:T(8,128)(2,1)} %bitcast.1), calls=%async_computation | async-start | bytes 327680 | tf_op jit(solution)/shard_map/all_to_all | solution.py:142
  50.1 82.3 %all-reduce.2.cloned.1.call-start = ((), (), s32[]{:S(2)}) async-start(), calls=%async_computation.3 | async-start | bytes 1310720 | tf_op jit(solution)/shard_map/psum | solution.py:148
  76.1 7.0 %slice-start.4 = ((s8[5242880]{0:T(1024)(128)(4,1)}), s8[4194304]{0:T(1024)(128)(4,1)S(1)}, s32[]{:S(2)}) async-start(s8[5242880]{0:T(1024)(128)(4,1)} %bitcast.49), calls=%async_computation.12 | async-start | bytes 8388608
  79.6 3.5 slice-start.5
  79.6 4.4 copy-start.4
  84.0 48.3 %copy-start.2 = (bf16[64,5120]{1,0:T(8,128)(2,1)S(1)}, bf16[64,5120]{1,0:T(8,128)(2,1)}, u32[]{:S(2)}) copy-start(bf16[64,5120]{1,0:T(8,128)(2,1)} %param.18) | copy-start | bytes 1966084
  84.0 49.8 %copy-start.5 = (f32[5120]{0:T(1024)S(1)}, f32[5120]{0:T(1024)}, u32[]{:S(2)}) copy-start(f32[5120]{0:T(1024)} %param.29) | copy-start | bytes 61444
  85.7 149.6 %all-gather.4.cloned.1.call-start = ((), (), s32[]{:S(2)}) async-start(), calls=%async_computation.4 | async-start | bytes 18432000 | tf_op jit(solution)/shard_map/all_gather | solution.py:153
  86.3 296.4 %all-gather.6.cloned.1.call-start = ((), (), s32[]{:S(2)}) async-start(), calls=%async_computation.5 | async-start | bytes 18432000 | tf_op jit(solution)/shard_map/all_gather | solution.py:155
  86.9 443.2 %all-gather.8.cloned.1.call-start = ((), (), s32[]{:S(2)}) async-start(), calls=%async_computation.6 | async-start | bytes 18432000 | tf_op jit(solution)/shard_map/all_gather | solution.py:158
  87.4 484.9 %reduce-scatter.2.cloned.1.call-start = ((), (), s32[]{:S(2)}) async-start(), calls=%async_computation.7 | async-start | bytes 819200 | tf_op jit(solution)/shard_map/reduce_scatter | solution.py:161
  382.7 18.1 %slice-start = ((s8[16384000]{0:T(1024)(128)(4,1)}), s8[4194304]{0:T(1024)(128)(4,1)S(1)}, s32[]{:S(2)}) async-start(s8[16384000]{0:T(1024)(128)(4,1)} %bitcast.47), calls=%async_computation.8 | async-start | bytes 8388608
  382.7 18.1 %slice-start.1 = ((s8[16384000]{0:T(1024)(128)(4,1)}), s8[4194304]{0:T(1024)(128)(4,1)S(1)}, s32[]{:S(2)}) async-start(s8[16384000]{0:T(1024)(128)(4,1)} %bitcast.47), calls=%async_computation.9 | async-start | bytes 8388608
  390.8 9.9 %slice-start.2 = ((s8[16384000]{0:T(1024)(128)(4,1)}), s8[4194304]{0:T(1024)(128)(4,1)S(1)}, s32[]{:S(2)}) async-start(s8[16384000]{0:T(1024)(128)(4,1)} %bitcast.47), calls=%async_computation.10 | async-start | bytes 8388608
  390.8 9.9 %slice-start.3 = ((s8[16384000]{0:T(1024)(128)(4,1)}), s8[3801088]{0:T(1024)(128)(4,1)S(1)}, s32[]{:S(2)}) async-start(s8[16384000]{0:T(1024)(128)(4,1)} %bitcast.47), calls=%async_computation.11 | async-start | bytes 7602176
  411.2 2.6 copy-start.7
  413.9 7.6 %copy-start.6 = (f32[3200]{0:T(1024)S(1)}, f32[3200]{0:T(1024)}, u32[]{:S(2)}) copy-start(f32[3200]{0:T(1024)} %param.33) | copy-start | bytes 38404
  530.1 10.3 %copy-start = (s32[800,5120]{1,0:T(8,128)S(1)}, s32[800,5120]{1,0:T(8,128)}, u32[]{:S(2)}) copy-start(s32[800,5120]{1,0:T(8,128)} %all-gather.8.cloned.1.call-done) | copy-start | bytes 49152004
  542.9 2.5 copy-start.3
Sparse Core Ops, SparseCore 0:
  85.8 46.4 all-reduce.1
  548.4 23.8 reduce-scatter.1
Sparse Core Ops, SparseCore 1:
  87.8 147.4 all-gather.3
  236.7 145.9 all-gather.5
  384.2 145.9 all-gather.7
where the time goes:
time: 589 us; the launch traced here: 582 us
  waiting for transfers between devices  376 us (64%)
  matrix products  85.7 us (15%)
  local copies, waits for them, and re-layouts  82.3 us (14%)
  between operations  16.1 us (3%)
  blocking collectives  9.25 us (2%)
  other arithmetic  7.26 us (1%)
    all_gather x1, waiting for transfers between devices, local(): lax.all_gather(w_up, ('grp', 'src'), axis=0, tiled=True)  139 us
    all_gather x1, waiting for transfers between devices, local(): lax.all_gather(w_down, ('grp', 'src'), axis=1, tiled=True)  91.5 us
    dot_general x20, matrix products, byte_product(): jnp.dot(activations[:, byte_index::4], unpack_bytes(packed, byte_index).a...  81.8 us
    all_gather x1, waiting for transfers between devices, local(): lax.all_gather(w_gate, ('grp', 'src'), axis=0, tiled=True)  74.5 us
    slice x16, local copies, waits for them, and re-layouts, byte_product(): activations[:, byte_index::4]  72.7 us
    psum x1, waiting for transfers between devices, local(): lax.psum(partial_value.astype(jnp.bfloat16), 'tp').astype(jnp.float32)  44.9 us
    reduce_scatter x1, waiting for transfers between devices, local(): lax.psum_scatter(down_terms.astype(jnp.bfloat16), 'tp', scatter_dimension...  24 us
  transfers between devices with their start and end apart: 6, of which 5 were waited for; matrix products, arithmetic and copies ran while one was open for 17% of the time, Pallas kernels for 0%

commit v1 on v0

--- a/solution.py
+++ b/solution.py
@@ -145,7 +145,9 @@
     )
     head_rows = lax.all_to_all(heads_out, "tp", split_axis=1, concat_axis=0, tiled=True)
     partial_value = byte_product(head_rows, w_out) * out_scale
-    attn_full = lax.psum(partial_value.astype(jnp.bfloat16), "tp").astype(jnp.float32)
+    attn_full = jnp.sum(lax.all_gather(partial_value.astype(jnp.bfloat16), "tp"), axis=0).astype(
+        jnp.float32
+    )
     mid_full = (residual + attn_full).astype(jnp.bfloat16)
     normed_mlp = normalize_rows(mid_full.astype(jnp.float32), mlp_gain).astype(jnp.bfloat16)
     mid_share = lax.dynamic_slice_in_dim(mid_full, tp_index * share_cols, share_cols, 1)

time: 589 us -> 629 us (1.068)
  waiting for transfers between devices: 376 us -> 414 us
    all_gather x1, waiting for transfers between devices: 74.5 us -> 120 us  [local(): lax.all_gather(w_gate, ('grp', 'src'), axis=0, tiled=True)]
    psum x1 -> x0, waiting for transfers between devices: 44.9 us -> none  [local(): lax.psum(partial_value.astype(jnp.bfloat16), 'tp').astype(jnp.float32)]
    all_gather x0 -> x1, waiting for transfers between devices: none -> 37.3 us  [local(): lax.all_gather(partial_value.astype(jnp.bfloat16), 'tp')]
  transfers between devices with their start and end apart: 6 -> 6, of which waited for: 5 -> 5; matrix products, arithmetic and copies ran while one was open for 17% -> 16% of each run, Pallas kernels for 0% -> 0%
where the time goes in v1:
time: 629 us; the launch traced here: 620 us
  waiting for transfers between devices  414 us (66%)
  matrix products  85.7 us (14%)
  local copies, waits for them, and re-layouts  82.3 us (13%)
  between operations  14.2 us (2%)
  blocking collectives  9.01 us (1%)
  other arithmetic  8.41 us (1%)
    all_gather x1, waiting for transfers between devices, local(): lax.all_gather(w_up, ('grp', 'src'), axis=0, tiled=True)  140 us
    all_gather x1, waiting for transfers between devices, local(): lax.all_gather(w_gate, ('grp', 'src'), axis=0, tiled=True)  120 us
    all_gather x1, waiting for transfers between devices, local(): lax.all_gather(w_down, ('grp', 'src'), axis=1, tiled=True)  91.6 us
    dot_general x20, matrix products, byte_product(): jnp.dot(activations[:, byte_index::4], unpack_bytes(packed, byte_index).a...  81.8 us
    slice x16, local copies, waits for them, and re-layouts, byte_product(): activations[:, byte_index::4]  72.4 us
    all_gather x1, waiting for transfers between devices, local(): lax.all_gather(partial_value.astype(jnp.bfloat16), 'tp')  37.3 us
    reduce_scatter x1, waiting for transfers between devices, local(): lax.psum_scatter(down_terms.astype(jnp.bfloat16), 'tp', scatter_dimension...  24 us
  transfers between devices with their start and end apart: 6, of which 5 were waited for; matrix products, arithmetic and copies ran while one was open for 16% of the time, Pallas kernels for 0%

profile of v1, /device:TPU:0, one launch (start us, length us, event | category | flops | bytes accessed | tf_op | source)
XLA Modules:
  0.0 619.5 jit_solution(17203893072316480046)
XLA Ops:
  9.2 6.5 %slice.73 = bf16[64,1280]{1,0:T(8,128)(2,1)S(1)} slice(bf16[64,5120]{1,0:T(8,128)(2,1)S(1)} %fusion.83), slice={[0:64:1], [0:5120:4]} | slice | bytes 327680 | tf_op jit(solution)/shard_map/slice | solution.py:24
  15.7 6.6 %slice.74 = bf16[64,1280]{1,0:T(8,128)(2,1)S(1)} slice(bf16[64,5120]{1,0:T(8,128)(2,1)S(1)} %fusion.83), slice={[0:64:1], [1:5120:4]} | slice | bytes 327680 | tf_op jit(solution)/shard_map/slice | solution.py:24
  22.3 6.5 %slice.75 = bf16[64,1280]{1,0:T(8,128)(2,1)S(1)} slice(bf16[64,5120]{1,0:T(8,128)(2,1)S(1)} %fusion.83), slice={[0:64:1], [2:5120:4]} | slice | bytes 327680 | tf_op jit(solution)/shard_map/slice | solution.py:24
  28.8 6.5 %slice.76 = bf16[64,1280]{1,0:T(8,128)(2,1)S(1)} slice(bf16[64,5120]{1,0:T(8,128)(2,1)S(1)} %fusion.83), slice={[0:64:1], [3:5120:4]} | slice | bytes 327680 | tf_op jit(solution)/shard_map/slice | solution.py:24
  35.3 4.0 fusion.50
  43.7 5.3 all-to-all-start
  51.9 4.0 reshape_squeeze.7
  61.4 9.0 %all_to_all.35 = bf16[16,4,1024]{2,0,1:T(8,128)(2,1)S(1)} all-to-all(bf16[16,4,1024]{2,0,1:T(8,128)(2,1)S(1)} %copy.28), channel_id=1, replica_groups=mesh['grp'=2,'tp'=4,'src'=4] {'tp'}, dimensions={1} | all-to-all | bytes 262144 | tf_op jit(solution)/shard_map/all_to_all | solution.py:146
  86.7 37.3 %all-gather.12.cloned.1.call-done = bf16[256,5120]{1,0:T(8,128)(2,1)} async-done(((bf16[64,5120]{1,0:T(8,128)(2,1)}), bf16[256,5120]{1,0:T(8,128)(2,1)}) %all-gather.12.cloned.1.call-update) | async-done | bytes 2621456 | tf_op jit(solution)/shard_map/all_gather | solution.py:148
  126.8 6.9 %slice.88 = bf16[64,1280]{1,0:T(8,128)(2,1)S(1)} slice(bf16[64,5120]{1,0:T(8,128)(2,1)S(1)} %fusion.80), slice={[0:64:1], [0:5120:4]} | slice | bytes 327680 | tf_op jit(solution)/shard_map/slice | solution.py:24
  133.8 6.6 %slice.89 = bf16[64,1280]{1,0:T(8,128)(2,1)S(1)} slice(bf16[64,5120]{1,0:T(8,128)(2,1)S(1)} %fusion.80), slice={[0:64:1], [1:5120:4]} | slice | bytes 327680 | tf_op jit(solution)/shard_map/slice | solution.py:24
  140.3 6.5 %slice.90 = bf16[64,1280]{1,0:T(8,128)(2,1)S(1)} slice(bf16[64,5120]{1,0:T(8,128)(2,1)S(1)} %fusion.80), slice={[0:64:1], [2:5120:4]} | slice | bytes 327680 | tf_op jit(solution)/shard_map/slice | solution.py:24
  146.8 6.7 %slice.91 = bf16[64,1280]{1,0:T(8,128)(2,1)S(1)} slice(bf16[64,5120]{1,0:T(8,128)(2,1)S(1)} %fusion.80), slice={[0:64:1], [3:5120:4]} | slice | bytes 327680 | tf_op jit(solution)/shard_map/slice | solution.py:24
  153.5 119.9 %all-gather.6.cloned.1.call-done = s32[1280,3200]{1,0:T(8,128)} async-done(((s32[160,3200]{1,0:T(8,128)}), s32[1280,3200]{1,0:T(8,128)}) %all-gather.6.cloned.1.call-update) | async-done | bytes 16384016 | tf_op jit(solution)/shard_map/all_gather | solution.py:155
  273.5 8.0 %fusion = f32[64,3200]{1,0:T(8,128)S(1)} fusion(bf16[64,1280]{1,0:T(8,128)(2,1)S(1)} %slice.88, s32[1280,3200]{1,0:T(8,128)} %all-gather.6.cloned.1.call-done), kind=kOutput, calls=%fused_computation.12 | convolution fusion | flops 536576000 | bytes 17367040 | tf_op jit(solution)/shard_map/dot_general | solution.py:23
  281.5 139.7 %all-gather.8.cloned.1.call-done = s32[1280,3200]{1,0:T(8,128)} async-done(((s32[160,3200]{1,0:T(8,128)}), s32[1280,3200]{1,0:T(8,128)}) %all-gather.8.cloned.1.call-update) | async-done | bytes 16384016 | tf_op jit(solution)/shard_map/all_gather | solution.py:157
  421.2 8.1 %fusion.4 = f32[64,3200]{1,0:T(8,128)S(1)} fusion(bf16[64,1280]{1,0:T(8,128)(2,1)S(1)} %slice.88, s32[1280,3200]{1,0:T(8,128)} %all-gather.8.cloned.1.call-done), kind=kOutput, calls=%fused_computation.16 | convolution fusion | flops 536576000 | bytes 17367040 | tf_op jit(solution)/shard_map/dot_general | solution.py:23
  429.3 9.9 %fusion.45 = f32[64,3200]{1,0:T(8,128)S(1)} fusion(f32[64,3200]{1,0:T(8,128)S(1)} %fusion, bf16[64,1280]{1,0:T(8,128)(2,1)S(1)} %slice.89, s32[1280,3200]{1,0:T(8,128)} %all-gather.6.cloned.1.call-done), kind=kOutput, calls=%fused_computation.68 | convolution fusion | flops 536780800 | bytes 18186240 | tf_op jit(solution)/shard_map/dot_general | solution.py:23
  441.7 8.1 %fusion.44 = f32[64,3200]{1,0:T(8,128)S(1)} fusion(f32[64,3200]{1,0:T(8,128)S(1)} %fusion.45, bf16[64,1280]{1,0:T(8,128)(2,1)S(1)} %slice.90, s32[1280,3200]{1,0:T(8,128)} %all-gather.6.cloned.1.call-done), kind=kOutput, calls=%fused_computation.67 | convolution fusion | flops 536780800 | bytes 18186240 | tf_op jit(solution)/shard_map/dot_general | solution.py:23
  452.4 7.6 %fusion.46 = f32[64,3200]{1,0:T(8,128)S(1)} fusion(f32[64,3200]{1,0:T(8,128)S(1)} %fusion.44, bf16[64,1280]{1,0:T(8,128)(2,1)S(1)} %slice.91, s32[1280,3200]{1,0:T(8,128)} %all-gather.6.cloned.1.call-done, f32[3200]{0:T(1024)S(1)} %copy-done.7), kind=kOutput, calls=%fused_computation.69 | convolution fusion | flops 536985600 | bytes 18199040 | tf_op jit(solution)/shard_map/dot_general | solution.py:23
  473.1 4.0 slice.95
  477.1 91.6 %all-gather.10.cloned.1.call-done = s32[800,5120]{1,0:T(8,128)} async-done(((s32[800,640]{1,0:T(8,128)}), s32[800,5120]{1,0:T(8,128)}) %all-gather.10.cloned.1.call-update) | async-done | bytes 16384016 | tf_op jit(solution)/shard_map/all_gather | solution.py:160
  568.7 8.2 %fusion.8 = f32[64,5120]{1,0:T(8,128)S(1)} fusion(bf16[64,800]{1,0:T(8,128)(2,1)S(1)} %slice.92, s32[800,5120]{1,0:T(8,128)} %all-gather.10.cloned.1.call-done), kind=kOutput, calls=%fused_computation.20 | convolution fusion | flops 536576000 | bytes 17797120 | tf_op jit(solution)/shard_map/dot_general | solution.py:23
  586.9 24.0 %reduce-scatter.2.cloned.1.call-done = bf16[64,1280]{1,0:T(8,128)(2,1)} async-done(((bf16[64,5120]{1,0:T(8,128)(2,1)}), bf16[64,1280]{1,0:T(8,128)(2,1)}) %reduce-scatter.2.cloned.1.call-update) | async-done | bytes 163856 | tf_op jit(solution)/shard_map/reduce_scatter | solution.py:163
  (106 shorter events, 63.9 us)
Async XLA Ops:
  35.3 4.7 copy-start.1
  40.1 2.1 copy-start.8
  41.1 8.0 %copy-start.11 = (s32[1,16]{1,0:T(1,128)S(1)}, s32[1,16]{1,0:T(1,128)}, u32[]{:S(2)}) copy-start(s32[1,16]{1,0:T(1,128)} %param.26) | copy-start | bytes 196
  43.7 12.7 %copy-start.9 = (f32[128]{0:T(128)S(1)}, f32[128]{0:T(128)}, u32[]{:S(2)}) copy-start(f32[128]{0:T(128)} %param.23) | copy-start | bytes 1540
  43.7 12.8 %copy-start.10 = (f32[128]{0:T(128)S(1)}, f32[128]{0:T(128)}, u32[]{:S(2)}) copy-start(f32[128]{0:T(128)} %param.22) | copy-start | bytes 1540
  43.7 12.3 %all-to-all-start = ((bf16[4,16,1280]{2,1,0:T(8,128)(2,1)}), bf16[4,16,1280]{2,1,0:T(8,128)(2,1)S(1)}, u32[]{:S(2)}, u32[]{:S(2)}) async-start(bf16[4,16,1280]{2,1,0:T(8,128)(2,1)} %bitcast.1), calls=%async_computation | async-start | bytes 327680 | tf_op jit(solution)/shard_map/all_to_all | solution.py:142
  49.1 74.9 %all-gather.12.cloned.1.call-start = ((), (), s32[]{:S(2)}) async-start(), calls=%async_computation.7 | async-start | bytes 3276800 | tf_op jit(solution)/shard_map/all_gather | solution.py:148
  75.1 7.0 %slice-start.4 = ((s8[5242880]{0:T(1024)(128)(4,1)}), s8[4194304]{0:T(1024)(128)(4,1)S(1)}, s32[]{:S(2)}) async-start(s8[5242880]{0:T(1024)(128)(4,1)} %bitcast.50), calls=%async_computation.12 | async-start | bytes 8388608
  78.6 3.5 slice-start.5
  78.6 4.4 copy-start.4
  84.6 41.6 %copy-start.2 = (bf16[64,5120]{1,0:T(8,128)(2,1)S(1)}, bf16[64,5120]{1,0:T(8,128)(2,1)}, u32[]{:S(2)}) copy-start(bf16[64,5120]{1,0:T(8,128)(2,1)} %param.18) | copy-start | bytes 1966084
  84.6 42.0 %copy-start.5 = (f32[5120]{0:T(1024)S(1)}, f32[5120]{0:T(1024)}, u32[]{:S(2)}) copy-start(f32[5120]{0:T(1024)} %param.29) | copy-start | bytes 61444
  84.6 188.9 %all-gather.6.cloned.1.call-start = ((), (), s32[]{:S(2)}) async-start(), calls=%async_computation.3 | async-start | bytes 18432000 | tf_op jit(solution)/shard_map/all_gather | solution.py:155
  85.4 335.8 %all-gather.8.cloned.1.call-start = ((), (), s32[]{:S(2)}) async-start(), calls=%async_computation.4 | async-start | bytes 18432000 | tf_op jit(solution)/shard_map/all_gather | solution.py:157
  86.1 482.6 %all-gather.10.cloned.1.call-start = ((), (), s32[]{:S(2)}) async-start(), calls=%async_computation.5 | async-start | bytes 18432000 | tf_op jit(solution)/shard_map/all_gather | solution.py:160
  86.7 524.3 %reduce-scatter.2.cloned.1.call-start = ((), (), s32[]{:S(2)}) async-start(), calls=%async_computation.6 | async-start | bytes 819200 | tf_op jit(solution)/shard_map/reduce_scatter | solution.py:163
  421.2 18.1 %slice-start = ((s8[16384000]{0:T(1024)(128)(4,1)}), s8[4194304]{0:T(1024)(128)(4,1)S(1)}, s32[]{:S(2)}) async-start(s8[16384000]{0:T(1024)(128)(4,1)} %bitcast.48), calls=%async_computation.8 | async-start | bytes 8388608
  421.2 18.1 %slice-start.1 = ((s8[16384000]{0:T(1024)(128)(4,1)}), s8[4194304]{0:T(1024)(128)(4,1)S(1)}, s32[]{:S(2)}) async-start(s8[16384000]{0:T(1024)(128)(4,1)} %bitcast.48), calls=%async_computation.9 | async-start | bytes 8388608
  429.3 10.0 %slice-start.2 = ((s8[16384000]{0:T(1024)(128)(4,1)}), s8[4194304]{0:T(1024)(128)(4,1)S(1)}, s32[]{:S(2)}) async-start(s8[16384000]{0:T(1024)(128)(4,1)} %bitcast.48), calls=%async_computation.10 | async-start | bytes 8388608
  429.3 10.0 %slice-start.3 = ((s8[16384000]{0:T(1024)(128)(4,1)}), s8[3801088]{0:T(1024)(128)(4,1)S(1)}, s32[]{:S(2)}) async-start(s8[16384000]{0:T(1024)(128)(4,1)} %bitcast.48), calls=%async_computation.11 | async-start | bytes 7602176
  449.7 2.6 copy-start.7
  452.4 7.6 %copy-start.6 = (f32[3200]{0:T(1024)S(1)}, f32[3200]{0:T(1024)}, u32[]{:S(2)}) copy-start(f32[3200]{0:T(1024)} %param.33) | copy-start | bytes 38404
  568.7 10.3 %copy-start = (s32[800,5120]{1,0:T(8,128)S(1)}, s32[800,5120]{1,0:T(8,128)}, u32[]{:S(2)}) copy-start(s32[800,5120]{1,0:T(8,128)} %all-gather.10.cloned.1.call-done) | copy-start | bytes 49152004
  581.5 2.5 copy-start.3
Sparse Core Ops, SparseCore 0:
  84.7 39.2 all-gather.11
  125.6 147.8 all-gather.5
  275.1 146.0 all-gather.7
  422.6 146.0 all-gather.9
  587.1 23.8 reduce-scatter.1
